TPU v7x, 128 devices: a whole 4x4x4 slice. The times are simulated.
128 devices in a mesh: dp: 1, sp: 128 (over z, y, x, core).
Axes of the slice: x: 4, y: 4, z: 4, core: 2. Of those that a mesh axis runs over, the one named last changes fastest.
Arguments:
- tokens: bfloat16 [32768, 2048], P(('dp', 'sp'))
- w_q: bfloat16 [2048, 32, 64], replicated
- w_k: bfloat16 [2048, 32, 64], replicated
- w_v: bfloat16 [2048, 32, 64], replicated
- w_o: bfloat16 [2048, 32, 64], replicated
- rand_idx: int32 [512, 12], P(('dp', 'sp'))
Outputs:
- output: bfloat16 [32768, 2048], P(('dp', 'sp'))
All inputs are finite; a program needn't handle non-finite values.
Results may differ from a plain program's by a relative error of at most 0.00323.
Values are sent between devices in bfloat16 or wider.
A program may use at most 1 GiB of HBM per device.

v0:
```python
import jax
import jax.numpy as jnp
from jax import lax
from jax.sharding import PartitionSpec as P

GLOB_BLOCKS = 2


def attend(q_loc, keys, values, valid, scale):
    num_keys, block = keys.shape[1], keys.shape[2]
    offsets = jnp.arange(block)
    causal = offsets[:, None] >= offsets[None, :]
    is_self = jnp.arange(num_keys) == GLOB_BLOCKS + 1
    mask = valid[:, None, :, None] & (~is_self[None, None, :, None] | causal[None, :, None, :])
    scores = jnp.einsum("iqhe,ikthe->ihqkt", q_loc, keys, preferred_element_type=jnp.float32) * scale
    scores = jnp.where(mask[:, None], scores, -jnp.inf)
    peak = jnp.max(scores, axis=(3, 4), keepdims=True)
    unnorm = jnp.exp(scores - peak)
    prob_bf = (unnorm / jnp.sum(unnorm, axis=(3, 4), keepdims=True)).astype(jnp.bfloat16)
    context = jnp.einsum("ihqkt,ikthe->iqhe", prob_bf, values, preferred_element_type=jnp.float32)
    return context.astype(jnp.bfloat16)


def solution(mesh):
    seq_devs = mesh.shape["sp"]
    shift_pairs = [(src, src + 1) for src in range(seq_devs - 1)]
    row_spec = P(("dp", "sp"), None)
    weight_spec = P(None, None, None)

    def local_fn(tokens, w_q, w_k, w_v, w_o, rand_idx):
        dev_pos = lax.axis_index("sp")
        blocks_dev, rand_count = rand_idx.shape
        block = tokens.shape[0] // blocks_dev
        heads, head_dim = w_q.shape[1], w_q.shape[2]

        def project(weight):
            proj = jnp.einsum("td,dhe->the", tokens, weight, preferred_element_type=jnp.float32)
            return proj.astype(jnp.bfloat16).reshape(blocks_dev, block, heads, head_dim)

        q_loc = project(w_q)
        k_loc = project(w_k)
        v_loc = project(w_v)
        first_row = dev_pos * blocks_dev
        rows = first_row + jnp.arange(blocks_dev)
        owner = rand_idx // blocks_dev
        hits = (owner[:, :, None] == jnp.arange(seq_devs)) & (rand_idx[:, :, None] >= 0)
        wanted = jnp.max(jnp.where(hits, rand_idx[:, :, None], -1), axis=(0, 1))
        asked = lax.all_to_all(wanted, "sp", 0, 0, tiled=True)
        serve_pos = jnp.clip(asked - first_row, 0, blocks_dev - 1)
        fetched_k = lax.all_to_all(jnp.take(k_loc, serve_pos, axis=0), "sp", 0, 0, tiled=True)
        fetched_v = lax.all_to_all(jnp.take(v_loc, serve_pos, axis=0), "sp", 0, 0, tiled=True)
        halo_k = lax.ppermute(k_loc[blocks_dev - 1], "sp", shift_pairs)
        halo_v = lax.ppermute(v_loc[blocks_dev - 1], "sp", shift_pairs)
        at_first = dev_pos == 0
        lead_k = lax.psum(jnp.where(at_first, k_loc[:GLOB_BLOCKS], jnp.zeros_like(k_loc[:GLOB_BLOCKS])), "sp")
        lead_v = lax.psum(jnp.where(at_first, v_loc[:GLOB_BLOCKS], jnp.zeros_like(v_loc[:GLOB_BLOCKS])), "sp")
        pool_pos = jnp.where(owner == dev_pos, rand_idx - first_row, blocks_dev + owner)
        pool_pos = jnp.clip(pool_pos, 0, blocks_dev + seq_devs - 1).reshape(-1)

        def key_set(own_blocks, halo, lead_blocks, fetched):
            pool = jnp.concatenate([own_blocks, fetched], axis=0)
            rand_part = jnp.take(pool, pool_pos, axis=0).reshape(blocks_dev, rand_count, block, heads, head_dim)
            prev_part = jnp.concatenate([halo[None], own_blocks[:-1]], axis=0)
            lead_part = jnp.broadcast_to(lead_blocks[None], (blocks_dev,) + lead_blocks.shape)
            return jnp.concatenate([lead_part, prev_part[:, None], own_blocks[:, None], rand_part], axis=1)

        keys = key_set(k_loc, halo_k, lead_k, fetched_k)
        values = key_set(v_loc, halo_v, lead_v, fetched_v)
        valid = jnp.concatenate([jnp.arange(GLOB_BLOCKS)[None, :] < rows[:, None], (rows - 1 >= GLOB_BLOCKS)[:, None], jnp.ones((blocks_dev, 1), jnp.bool_), rand_idx >= 0], axis=1)
        context = attend(q_loc, keys, values, valid, head_dim ** -0.5)
        context = context.reshape(blocks_dev * block, heads, head_dim)
        result = jnp.einsum("the,dhe->td", context, w_o, preferred_element_type=jnp.float32)
        return result.astype(jnp.bfloat16)

    return jax.shard_map(local_fn, mesh=mesh, in_specs=(row_spec, weight_spec, weight_spec, weight_spec, weight_spec, row_spec), out_specs=row_spec, check_vma=False)
```

profile of v0, /device:TPU:18, one launch (start us, length us, event | category | flops | bytes accessed | tf_op | source)
XLA Modules:
  0.0 1963.4 jit_solution(10653097152367737850)
XLA Ops:
  10.4 10.3 all-to-all-start
  20.8 5.8 fusion.25
  26.5 7.1 fusion.27
  34.8 3.9 copy.96
  42.2 4.7 copy.97
  49.3 22.2 %gather_fusion = bf16[128,64,32,64]{3,2,1,0:T(8,128)(2,1)} fusion(bf16[4,64,32,64]{3,2,1,0:T(8,128)(2,1)S(1)} %bitcast.81, s32[1024]{0:T(1024)S(1)} %pad_clamp_fusion.1), kind=kCustom, calls=%fused_computation.clone | custom fusion | bytes 67109376 | tf_op jit(solution)/shard_map/jit(_take)/gather | solution.py:51
  71.4 23.8 %gather_fusion.2 = bf16[128,64,32,64]{3,2,1,0:T(8,128)(2,1)} fusion(bf16[4,64,32,64]{3,2,1,0:T(8,128)(2,1)} %bitcast.83, s32[1024]{0:T(1024)S(1)} %pad_clamp_fusion.1), kind=kCustom, calls=%fused_computation.2.clone | custom fusion | bytes 67109376 | tf_op jit(solution)/shard_map/jit(_take)/gather | solution.py:50
  95.2 86.0 %broadcast_select_fusion.1 = (bf16[128,64,32,64]{3,2,1,0:T(8,128)(2,1)}, bf16[128,64,32,64]{3,2,1,0:T(8,128)(2,1)}) fusion(bf16[128,64,32,64]{3,2,1,0:T(8,128)(2,1)} %gather_fusion, pred[128]{0:T(512)(128)(4,1)S(1)} %compare_and_fusion.1, bf16[128,64,32,64]{3,2,1,0:T(8,128)(2,1)} %gather_fusion.2), kind=kLoop, calls=%fused_computation.10 | loop fusion | flops 33554432 | bytes 134217856 | tf_op jit(solution)/shard_map/jit(_take)/select_n | solution.py:51
  181.2 103.2 %reshape.164 = bf16[128,2,65536]{2,1,0:T(2,128)(2,1)} reshape(bf16[128,64,32,64]{3,2,1,0:T(8,128)(2,1)} %get-tuple-element.14) | data formatting | bytes 67108864
  284.4 10.0 all-to-all-start.2
  294.4 103.2 %reshape.166 = bf16[128,2,65536]{2,1,0:T(2,128)(2,1)} reshape(bf16[128,64,32,64]{3,2,1,0:T(8,128)(2,1)} %get-tuple-element.13) | data formatting | bytes 67108864
  397.6 403.9 %all-to-all-done.2 = bf16[128,2,65536]{2,1,0:T(2,128)(2,1)} async-done(((bf16[128,2,65536]{2,1,0:T(2,128)(2,1)}), bf16[128,2,65536]{2,1,0:T(2,128)(2,1)}, u32[]{:S(2)}, u32[]{:S(2)}) %all-to-all-start.2) | async-done | bytes 33554464 | tf_op jit(solution)/shard_map/all_to_all | solution.py:50
  801.5 35.3 %all-to-all-start.1 = ((bf16[128,2,65536]{2,1,0:T(2,128)(2,1)}), bf16[128,2,65536]{2,1,0:T(2,128)(2,1)}, u32[]{:S(2)}, u32[]{:S(2)}) async-start(bf16[128,2,65536]{2,1,0:T(2,128)(2,1)} %reshape.166), calls=%async_computation.1 | async-start | bytes 67108864 | tf_op jit(solution)/shard_map/all_to_all | solution.py:51
  854.1 6.8 bitcast_convert_fusion.1
  870.4 4.3 copy.89
  874.7 4.4 reshape.104
  887.3 494.0 %collective-permute-done.1 = bf16[64,32,64]{0,2,1:T(8,128)(2,1)} collective-permute-done((bf16[64,32,64]{0,2,1:T(8,128)(2,1)}, bf16[64,32,64]{0,2,1:T(8,128)(2,1)}, u32[]{:S(2)}, u32[]{:S(2)}) %collective-permute-start.1) | collective-permute-done | bytes 262176 | tf_op jit(solution)/shard_map/ppermute | solution.py:52
  1389.7 3.6 copy.83
  1395.8 100.5 %reshape.165 = bf16[128,64,32,64]{3,2,1,0:T(8,128)(2,1)} reshape(bf16[128,2,65536]{2,1,0:T(2,128)(2,1)} %all-to-all-done.2) | data formatting | bytes 67108864
  1496.3 45.7 %pad_maximum_fusion.1 = bf16[132,64,32,64]{3,2,1,0:T(8,128)(2,1)} fusion(bf16[128,64,32,64]{3,2,1,0:T(8,128)(2,1)} %reshape.165, bf16[4,64,32,64]{3,2,1,0:T(8,128)(2,1)S(1)} %bitcast.84), kind=kLoop, calls=%fused_computation.5 | loop fusion | flops 17301504 | bytes 69206016 | tf_op jit(solution)/shard_map/concatenate | solution.py:61
  1542.0 100.5 %reshape.167 = bf16[128,64,32,64]{3,2,1,0:T(8,128)(2,1)} reshape(bf16[128,2,65536]{2,1,0:T(2,128)(2,1)} %all-to-all-done.1) | data formatting | bytes 67108864
  1642.5 45.7 %pad_maximum_fusion = bf16[132,64,32,64]{3,2,1,0:T(8,128)(2,1)} fusion(bf16[128,64,32,64]{3,2,1,0:T(8,128)(2,1)} %reshape.167, bf16[4,64,32,64]{3,2,1,0:T(8,128)(2,1)S(1)} %bitcast.82), kind=kLoop, calls=%fused_computation.4 | loop fusion | flops 17301504 | bytes 69206016 | tf_op jit(solution)/shard_map/concatenate | solution.py:61
  1688.2 18.7 gather_fusion.3
  1706.9 18.8 gather_fusion.1
  1725.7 33.0 %broadcast_select_fusion.3 = (bf16[48,64,32,64]{3,2,1,0:T(8,128)(2,1)}, bf16[48,64,32,64]{3,2,1,0:T(8,128)(2,1)}) fusion(bf16[48,64,32,64]{3,2,1,0:T(8,128)(2,1)} %gather_fusion.1, pred[48]{0:T(512)(128)(4,1)S(1)} %copy-done.15, bf16[48,64,32,64]{3,2,1,0:T(8,128)(2,1)} %gather_fusion.3), kind=kLoop, calls=%fused_computation.24 | loop fusion | flops 12582912 | bytes 50331696 | tf_op jit(solution)/shard_map/jit(_take)/select_n | solution.py:62
  1758.7 25.1 %copy.90 = bf16[4,12,64,32,64]{4,2,1,3,0:T(8,128)(2,1)} copy(bf16[4,12,64,32,64]{4,3,2,1,0:T(8,128)(2,1)} %bitcast.87) | data formatting | bytes 25165824 | tf_op jit(solution)/shard_map/reshape | solution.py:62
  1783.8 32.5 %copy.82 = bf16[4,12,64,32,64]{2,4,1,3,0:T(8,128)(2,1)} copy(bf16[4,12,64,32,64]{4,3,2,1,0:T(8,128)(2,1)} %bitcast.86) | data formatting | bytes 25165824 | tf_op jit(solution)/shard_map/reshape | solution.py:62
  1819.4 22.8 %pad_maximum_fusion.2 = bf16[4,16,64,32,64]{4,2,1,3,0:T(8,128)(2,1)} fusion(bf16[4,12,64,32,64]{4,2,1,3,0:T(8,128)(2,1)} %copy.90, bf16[4,1,64,32,64]{4,2,1,3,0:T(8,128)(2,1)} %copy.89, bf16[4,1,64,32,64]{4,2,1,3,0:T(8,128)(2,1)} %maximum_bitcast_fusion.1, bf16[4,2,64,32,64]{4,2,1,3,0:T(8,128)(2,1)} %broadcast_in_dim.87), kind=kLoop, calls=%fused_computation.21 | loop fusion | flops 25165824 | bytes 33554432 | tf_op jit(solution)/shard_map/concatenate | solution.py:65
  1842.2 33.7 %fusion = (f32[4,32,64]{2,1,0:T(8,128)S(1)}, f32[4,32,64,1024]{2,3,1,0}) fusion(pred[4,64,16,64]{1,3,2,0:T(8,128)(4,1)S(1)} %copy-done.8, bf16[4,32,64,1024]{2,3,1,0:T(8,128)(2,1)} %bitcast.85, bf16[4,64,32,64]{1,0,3,2:T(4,128)(2,1)S(1)} %copy-done.7), kind=kOutput, calls=%fused_computation.11 | convolution fusion | flops 1098899456 | bytes 51675136
  1876.0 21.5 %fusion.1 = f32[4,32,64]{2,1,0:T(8,128)S(1)} fusion(f32[4,32,64,1024]{2,3,1,0} %get-tuple-element.16, f32[4,32,64]{2,1,0:T(8,128)S(1)} %get-tuple-element.15, pred[4,64,16,64]{1,3,2,0:T(8,128)(4,1)S(1)} %copy-done.8), kind=kLoop, calls=%fused_computation.12 | loop fusion | flops 33546240 | bytes 33882112 | tf_op jit(solution)/shard_map/reduce_sum | solution.py:19
  1900.6 42.9 %fusion.16 = bf16[4,64,32,64]{1,3,2,0:T(8,128)(2,1)} fusion(f32[4,32,64,1024]{2,3,1,0} %get-tuple-element.16, f32[4,32,64]{2,1,0:T(8,128)S(1)} %fusion.1, f32[4,32,64]{2,1,0:T(8,128)S(1)} %get-tuple-element.15, pred[4,64,16,64]{1,3,2,0:T(8,128)(4,1)S(1)} %copy-done.9, bf16[4,12,64,32,64]{2,4,1,3,0:T(8,128)(2,1)} %copy.82, ...), kind=kOutput, calls=%fused_computation.32 | convolution fusion | flops 1141374976 | bytes 51707904 | tf_op jit(solution)/shard_map/ihqkt,ikthe->iqhe/dot_general | solution.py:20
  1949.3 7.0 fusion.11
  (87 shorter events, 68.4 us)
Async XLA Ops:
  6.5 14.2 copy-start
  7.3 26.3 %copy-start.13 = (pred[4,12]{1,0:T(4,128)(4,1)}, pred[4,12]{1,0:T(4,128)(4,1)S(1)}, u32[]{:S(2)}) copy-start(pred[4,12]{1,0:T(4,128)(4,1)S(1)} %broadcast_compare_fusion) | copy-start | bytes 148
  10.4 36.4 %all-to-all-start = ((s32[128,1,1]{2,1,0:T(1,128)}), s32[128,1,1]{2,1,0:T(1,128)S(1)}, u32[]{:S(2)}, u32[]{:S(2)}) async-start(s32[128,1,1]{2,1,0:T(1,128)} %copy.78), calls=%async_computation | async-start | bytes 131072 | tf_op jit(solution)/shard_map/all_to_all | solution.py:48
  38.7 32.7 %copy-start.2 = (bf16[256,32,64]{2,1,0:T(8,128)(2,1)}, bf16[256,32,64]{2,1,0:T(8,128)(2,1)S(1)}, u32[]{:S(2)}) copy-start(bf16[256,32,64]{2,1,0:T(8,128)(2,1)S(1)} %copy.96) | copy-start | bytes 3145732
  284.4 517.1 %all-to-all-start.2 = ((bf16[128,2,65536]{2,1,0:T(2,128)(2,1)}), bf16[128,2,65536]{2,1,0:T(2,128)(2,1)}, u32[]{:S(2)}, u32[]{:S(2)}) async-start(bf16[128,2,65536]{2,1,0:T(2,128)(2,1)} %reshape.164), calls=%async_computation.2 | async-start | bytes 67108864 | tf_op jit(solution)/shard_map/all_to_all | solution.py:50
  397.6 439.3 %copy-start.6 = (bf16[256,32,64]{0,2,1:T(8,128)(2,1)S(1)}, bf16[256,32,64]{0,2,1:T(8,128)(2,1)}, u32[]{:S(2)}) copy-start(bf16[256,32,64]{0,2,1:T(8,128)(2,1)} %convert_element_type.23) | copy-start | bytes 3145732
  397.6 442.4 %copy-start.5 = (bf16[256,32,64]{0,2,1:T(8,128)(2,1)S(1)}, bf16[256,32,64]{0,2,1:T(8,128)(2,1)}, u32[]{:S(2)}) copy-start(bf16[256,32,64]{0,2,1:T(8,128)(2,1)} %convert_element_type.21) | copy-start | bytes 3145732
  397.6 454.9 %copy-start.12 = (s32[4,12]{1,0:T(4,128)S(1)}, s32[4,12]{1,0:T(4,128)}, u32[]{:S(2)}) copy-start(s32[4,12]{1,0:T(4,128)} %get-tuple-element.9) | copy-start | bytes 580
  397.6 455.2 %copy-start.14 = (pred[4,12]{1,0:T(4,128)(4,1)S(1)}, pred[4,12]{1,0:T(4,128)(4,1)}, u32[]{:S(2)}) copy-start(pred[4,12]{1,0:T(4,128)(4,1)} %copy-done.13) | copy-start | bytes 148
  801.5 740.5 %all-to-all-start.1 = ((bf16[128,2,65536]{2,1,0:T(2,128)(2,1)}), bf16[128,2,65536]{2,1,0:T(2,128)(2,1)}, u32[]{:S(2)}, u32[]{:S(2)}) async-start(bf16[128,2,65536]{2,1,0:T(2,128)(2,1)} %reshape.166), calls=%async_computation.1 | async-start | bytes 67108864 | tf_op jit(solution)/shard_map/all_to_all | solution.py:51
  836.9 552.8 %all-reduce.3.cloned.1.call-start = ((), (), s32[]{:S(2)}) async-start(), calls=%async_computation.3 | async-start | bytes 4194304 | tf_op jit(solution)/shard_map/psum | solution.py:55
  837.9 543.4 %collective-permute-start.1 = (bf16[64,32,64]{0,2,1:T(8,128)(2,1)}, bf16[64,32,64]{0,2,1:T(8,128)(2,1)}, u32[]{:S(2)}, u32[]{:S(2)}) collective-permute-start(bf16[64,32,64]{0,2,1:T(8,128)(2,1)} %slice.48), channel_id=1, source_target_pairs={{0,1},{1,2},{2,3},{3,4},{4,5},{5,6},{6,7},{7,8},{8,9},{9,10},{10,1... | collective-permute-start | bytes 786440 | tf_op jit(solution)/shard_map/ppermute | solution.py:52
  841.0 546.0 %collective-permute-start = (bf16[64,32,64]{0,2,1:T(8,128)(2,1)}, bf16[64,32,64]{0,2,1:T(8,128)(2,1)}, u32[]{:S(2)}, u32[]{:S(2)}) collective-permute-start(bf16[64,32,64]{0,2,1:T(8,128)(2,1)} %slice.45), channel_id=1, source_target_pairs={{0,1},{1,2},{2,3},{3,4},{4,5},{5,6},{6,7},{7,8},{8,9},{9,10},{10,1... | collective-permute-start | bytes 786440 | tf_op jit(solution)/shard_map/ppermute | solution.py:53
  1395.8 100.5 %copy-start.4 = (bf16[256,32,64]{2,1,0:T(8,128)(2,1)S(1)}, bf16[256,32,64]{2,1,0:T(8,128)(2,1)}, u32[]{:S(2)}) copy-start(bf16[256,32,64]{2,1,0:T(8,128)(2,1)} %copy.97) | copy-start | bytes 3145732
  1542.0 100.5 %copy-start.3 = (bf16[256,32,64]{2,1,0:T(8,128)(2,1)S(1)}, bf16[256,32,64]{2,1,0:T(8,128)(2,1)}, u32[]{:S(2)}) copy-start(bf16[256,32,64]{2,1,0:T(8,128)(2,1)} %copy-done.2) | copy-start | bytes 3145732
  1706.9 18.8 copy-start.15
  1783.8 32.5 %copy-start.11 = (bf16[2,64,32,64]{3,1,0,2:T(8,128)(2,1)S(1)}, bf16[2,64,32,64]{3,1,0,2:T(8,128)(2,1)}, u32[]{:S(2)}) copy-start(bf16[2,64,32,64]{3,1,0,2:T(8,128)(2,1)} %copy.83) | copy-start | bytes 1572868
  1819.4 22.8 %copy-start.7 = (bf16[4,64,32,64]{1,0,3,2:T(4,128)(2,1)S(1)}, bf16[4,64,32,64]{1,0,3,2:T(4,128)(2,1)}, u32[]{:S(2)}) copy-start(bf16[4,64,32,64]{1,0,3,2:T(4,128)(2,1)} %reshape.104) | copy-start | bytes 3145732
  1819.4 22.8 %copy-start.8 = (pred[4,64,16,64]{1,3,2,0:T(8,128)(4,1)S(1)}, pred[4,64,16,64]{1,3,2,0:T(8,128)(4,1)}, u32[]{:S(2)}) copy-start(pred[4,64,16,64]{1,3,2,0:T(8,128)(4,1)} %broadcast_and_fusion) | copy-start | bytes 786436
  1876.0 21.6 %copy-start.10 = (bf16[2,64,32,64]{1,3,0,2:T(8,128)(2,1)S(1)}, bf16[2,64,32,64]{1,3,0,2:T(8,128)(2,1)}, u32[]{:S(2)}) copy-start(bf16[2,64,32,64]{1,3,0,2:T(8,128)(2,1)} %copy.72) | copy-start | bytes 1572868
  1876.0 24.7 %copy-start.9 = (pred[4,64,16,64]{1,3,2,0:T(8,128)(4,1)S(1)}, pred[4,64,16,64]{1,3,2,0:T(8,128)(4,1)}, u32[]{:S(2)}) copy-start(pred[4,64,16,64]{1,3,2,0:T(8,128)(4,1)} %broadcast_and_fusion) | copy-start | bytes 786436
  1900.6 55.7 %copy-start.1 = (bf16[256,2048]{1,0:T(8,128)(2,1)S(1)}, bf16[256,2048]{1,0:T(8,128)(2,1)}, u32[]{:S(2)}) copy-start(bf16[256,2048]{1,0:T(8,128)(2,1)} %param.10) | copy-start | bytes 3145732
Sparse Core Ops, SparseCore 0:
  852.6 438.2 all-reduce.2
where the time goes:
time: 1990 us; the launch traced here: 1960 us
  waiting for transfers between devices  899 us (45%)
  local copies, waits for them, and re-layouts  613 us (31%)
  other arithmetic  273 us (14%)
  matrix products  103 us (5%)
  starting transfers between devices  61 us (3%)
    ppermute x1, waiting for transfers between devices, local_fn(): halo_k = lax.ppermute(k_loc[blocks_dev - 1], 'sp', shift_pairs)  494 us
    unnamed x37, local copies, waits for them, and re-layouts  408 us
    all_to_all x1, waiting for transfers between devices, local_fn(): lax.all_to_all(jnp.take(k_loc, serve_pos, axis=0), 'sp', 0, 0, tiled=True)  404 us
    concatenate x2, other arithmetic, key_set(): pool = jnp.concatenate([own_blocks, fetched], axis=0)  91.3 us
    select_n x2, other arithmetic, local_fn(): jnp.take(v_loc, serve_pos, axis=0)  86 us
    reshape x2, local copies, waits for them, and re-layouts, key_set(): jnp.take(pool, pool_pos, axis=0)  57.6 us
    unnamed x4, matrix products  53.4 us
    dot_general x1, matrix products, attend(): jnp.einsum('ihqkt,ikthe->iqhe', prob_bf, values, preferred_element_type=j...  42.9 us
  transfers between devices with their start and end apart: 6, of which 3 were waited for; matrix products, arithmetic and copies ran while one was open for 17% of the time, Pallas kernels for 0%

commit v1 on v0

v1 whole, which is shorter than its diff:
```python
import functools

import jax
import jax.numpy as jnp
from jax import lax
from jax.experimental import pallas as pl
from jax.experimental.pallas import tpu as pltpu
from jax.sharding import PartitionSpec as P

GLOB_BLOCKS = 2
HEAD_GROUP = 4
TILE_BLOCKS = 8
COLS = 256
LOG2E = 1.4426950408889634


def attend_kernel(
    proj_steps, blocks_dev, num_keys, block, head_dim,
    ids_ref, count_ref, slots_ref,
    q_ref, bias_ref, tok_ref, wk_ref, wv_ref, wo_ref, kn_ref, vn_ref,
    out_ref,
    kpool, vpool, xbuf, wbuf, ctx,
    x_sem, w_sem, near_sem,
):
    step = pl.program_id(0)
    used = count_ref[0]
    far = proj_steps * TILE_BLOCKS
    width = q_ref.shape[1]

    def x_copy(at, g):
        return pltpu.make_async_copy(tok_ref.at[ids_ref[at * TILE_BLOCKS + g]], xbuf.at[lax.rem(at, 2), g], x_sem.at[lax.rem(at, 2), g])

    def w_copy(src, which):
        return pltpu.make_async_copy(src, wbuf.at[which], w_sem.at[which])

    def near_copies():
        return (
            pltpu.make_async_copy(kn_ref, kpool.at[pl.ds(far, blocks_dev)], near_sem.at[0]),
            pltpu.make_async_copy(vn_ref, vpool.at[pl.ds(far, blocks_dev)], near_sem.at[1]),
        )

    @pl.when(step == 0)
    def _():
        for g in range(TILE_BLOCKS):
            x_copy(0, g).start()
        w_copy(wk_ref, 0).start()
        w_copy(wv_ref, 1).start()
        for copy in near_copies():
            copy.start()

    @pl.when(step + 1 < used)
    def _():
        for g in range(TILE_BLOCKS):
            x_copy(step + 1, g).start()

    def fill(pool, which):
        def column(c, carry):
            at = pl.ds(pl.multiple_of(c * COLS, COLS), COLS)
            tok = xbuf[lax.rem(step, 2)].reshape(TILE_BLOCKS * block, -1)
            proj = jnp.dot(tok, wbuf[which, :, at], preferred_element_type=jnp.float32)
            pool[pl.ds(step * TILE_BLOCKS, TILE_BLOCKS), :, at] = proj.astype(jnp.bfloat16).reshape(TILE_BLOCKS, block, COLS)
            return carry

        lax.fori_loop(0, width // COLS, column, 0)

    @pl.when(step < used)
    def _():
        for g in range(TILE_BLOCKS):
            x_copy(step, g).wait()

        @pl.when(step == 0)
        def _():
            w_copy(wk_ref, 0).wait()

        fill(kpool, 0)

        @pl.when(step == 0)
        def _():
            w_copy(wv_ref, 1).wait()

        fill(vpool, 1)

    @pl.when(step == proj_steps)
    def _():
        w_copy(wo_ref, 0).start()
        for copy in near_copies():
            copy.wait()

    @pl.when(step >= proj_steps)
    def _():
        row = step - proj_steps
        wide = HEAD_GROUP * head_dim
        rows = HEAD_GROUP * block
        keys = num_keys * block
        factor = head_dim ** -0.5 * LOG2E
        lane_head = lax.broadcasted_iota(jnp.int32, (block, wide), 1) // head_dim
        q_pos = lax.rem(lax.broadcasted_iota(jnp.int32, (rows, 2 * block), 0), block)
        k_pos = lax.broadcasted_iota(jnp.int32, (rows, 2 * block), 1)
        causal = (k_pos <= q_pos) | (k_pos >= block)
        bias = bias_ref[0]
        slots = [slots_ref[row * num_keys + j] for j in range(num_keys)]

        def heads(g, carry):
            lanes = pl.ds(pl.multiple_of(g * wide, wide), wide)
            q = q_ref[:, lanes]
            zero = jnp.zeros_like(q)
            q_diag = jnp.concatenate([jnp.where(lane_head == h, q, zero) for h in range(HEAD_GROUP)], axis=0)
            k = jnp.concatenate([kpool[slot, :, lanes] for slot in slots], axis=0)
            scores = lax.dot_general(q_diag, k, (((1,), (1,)), ((), ())), preferred_element_type=jnp.float32) + bias
            own = jnp.where(causal, scores[:, : 2 * block], -jnp.inf)
            scores = jnp.concatenate([own, scores[:, 2 * block :]], axis=1)
            peak = jnp.max(scores, axis=1, keepdims=True)
            unnorm = jnp.exp2((scores - peak) * factor)
            total = jnp.sum(unnorm, axis=1, keepdims=True)
            prob = (unnorm * (1.0 / total)).astype(jnp.bfloat16)
            v = jnp.concatenate([vpool[slot, :, lanes] for slot in slots], axis=0)
            mixed = jnp.dot(prob, v, preferred_element_type=jnp.float32)
            picked = mixed[:block]
            for h in range(1, HEAD_GROUP):
                picked = jnp.where(lane_head == h, mixed[h * block : (h + 1) * block], picked)
            ctx[pl.ds(pl.multiple_of(row * block, block), block), lanes] = picked.astype(jnp.bfloat16)
            return carry

        lax.fori_loop(0, width // wide, heads, 0)

    @pl.when(step == proj_steps + blocks_dev - 1)
    def _():
        w_copy(wo_ref, 0).wait()

        def column(c, carry):
            at = pl.ds(pl.multiple_of(c * COLS, COLS), COLS)
            out_ref[:, at] = jnp.dot(ctx[...], wbuf[0, :, at], preferred_element_type=jnp.float32).astype(jnp.bfloat16)
            return carry

        lax.fori_loop(0, out_ref.shape[1] // COLS, column, 0)


def attend(ids, count, slots, q, bias, tok, wk, wv, wo, k_near, v_near, head_dim):
    blocks_dev, block, width = k_near.shape
    model = wo.shape[1]
    proj_steps = ids.shape[0] // TILE_BLOCKS
    num_keys = slots.shape[0] // blocks_dev
    pool = proj_steps * TILE_BLOCKS + blocks_dev
    any_spec = pl.BlockSpec(memory_space=pl.ANY)
    row_of = lambda i: jnp.maximum(i - proj_steps, 0)
    grid_spec = pltpu.PrefetchScalarGridSpec(
        num_scalar_prefetch=3,
        grid=(proj_steps + blocks_dev,),
        in_specs=[
            pl.BlockSpec((block, width), lambda i, *_: (row_of(i), 0)),
            pl.BlockSpec((1, 1, num_keys * block), lambda i, *_: (row_of(i), 0, 0)),
        ] + [any_spec] * 6,
        out_specs=pl.BlockSpec((blocks_dev * block, model), lambda i, *_: (0, 0)),
        scratch_shapes=[
            pltpu.VMEM((pool, block, width), jnp.bfloat16),
            pltpu.VMEM((pool, block, width), jnp.bfloat16),
            pltpu.VMEM((2, TILE_BLOCKS, block, model), jnp.bfloat16),
            pltpu.VMEM((2, model, width), jnp.bfloat16),
            pltpu.VMEM((blocks_dev * block, width), jnp.bfloat16),
            pltpu.SemaphoreType.DMA((2, TILE_BLOCKS)),
            pltpu.SemaphoreType.DMA((2,)),
            pltpu.SemaphoreType.DMA((2,)),
        ],
    )
    return pl.pallas_call(
        functools.partial(attend_kernel, proj_steps, blocks_dev, num_keys, block, head_dim),
        grid_spec=grid_spec,
        out_shape=jax.ShapeDtypeStruct((blocks_dev * block, model), jnp.bfloat16),
        compiler_params=pltpu.CompilerParams(dimension_semantics=("arbitrary",), vmem_limit_bytes=67043328),
        cost_estimate=pl.CostEstimate(flops=70_000_000_000, bytes_accessed=60_000_000, transcendentals=8_000_000),
        name="attend",
    )(ids, count, slots, q, bias, tok, wk, wv, wo, k_near, v_near)


def solution(mesh):
    seq_devs = mesh.shape["sp"]
    row_spec = P(("dp", "sp"), None)
    weight_spec = P(None, None, None)

    def local_fn(tokens, w_q, w_k, w_v, w_o, rand_idx):
        me = lax.axis_index("sp")
        blocks_dev, rand_count = rand_idx.shape
        block = tokens.shape[0] // blocks_dev
        model, heads, head_dim = w_q.shape
        width = heads * head_dim
        all_tok = lax.all_gather(tokens, "sp", axis=0, tiled=True).reshape(seq_devs * blocks_dev, block, model)

        wq, wk, wv = (w.reshape(model, width) for w in (w_q, w_k, w_v))
        wo = jnp.transpose(w_o, (1, 2, 0)).reshape(width, model)

        def project(weight):
            return jnp.dot(tokens, weight, preferred_element_type=jnp.float32).astype(jnp.bfloat16)

        q_loc = project(wq)
        k_near = project(wk).reshape(blocks_dev, block, width)
        v_near = project(wv).reshape(blocks_dev, block, width)

        first_row = me * blocks_dev
        local = jnp.arange(blocks_dev)
        rows = first_row + local
        devs = jnp.arange(seq_devs)
        owner = rand_idx // blocks_dev
        hits = (owner[:, :, None] == devs) & (rand_idx[:, :, None] >= 0)
        wanted = jnp.max(jnp.where(hits, rand_idx[:, :, None], -1), axis=(0, 1))
        need = ((wanted >= 0) & (devs != me)).astype(jnp.int32)
        fixed = GLOB_BLOCKS + 1
        slot_of = fixed + jnp.cumsum(need) - need
        steps = -(-(fixed + blocks_dev * rand_count) // TILE_BLOCKS)
        pool_rows = steps * TILE_BLOCKS
        total = fixed + jnp.sum(need)
        used = (total + TILE_BLOCKS - 1) // TILE_BLOCKS
        place = jnp.arange(pool_rows)
        ids = jnp.sum(jnp.where((slot_of[None, :] == place[:, None]) & (need[None, :] > 0), wanted[None, :], 0), axis=1)
        ids = ids + jnp.where(place < GLOB_BLOCKS, place, jnp.where(place == GLOB_BLOCKS, jnp.maximum(first_row - 1, 0), 0))
        far_pos = jnp.sum(jnp.where(hits, slot_of, 0), axis=2)
        rand_pos = jnp.where(rand_idx < 0, pool_rows, jnp.where(owner == me, pool_rows + rand_idx - first_row, far_pos))
        prev = jnp.where(local == 0, GLOB_BLOCKS, pool_rows + local - 1)
        lead = jnp.broadcast_to(jnp.arange(GLOB_BLOCKS), (blocks_dev, GLOB_BLOCKS))
        slots = jnp.concatenate([pool_rows + local[:, None], prev[:, None], lead, rand_pos], axis=1).reshape(-1)
        valid = jnp.concatenate([jnp.ones((blocks_dev, 1), jnp.bool_), (rows - 1 >= GLOB_BLOCKS)[:, None], jnp.arange(GLOB_BLOCKS)[None, :] < rows[:, None], rand_idx >= 0], axis=1)
        bias = jnp.where(jnp.repeat(valid, block, axis=1), 0.0, -jnp.inf).astype(jnp.float32)[:, None, :]
        i32 = lambda a: a.astype(jnp.int32)
        return attend(i32(ids), i32(used)[None], i32(slots), q_loc, bias, all_tok, wk, wv, wo, k_near, v_near, head_dim)

    return jax.shard_map(local_fn, mesh=mesh, in_specs=(row_spec, weight_spec, weight_spec, weight_spec, weight_spec, row_spec), out_specs=row_spec, check_vma=False)
```

time: 1990 us -> 417 us (0.21)
  the two profiles are of different devices: /device:TPU:18 before, /device:TPU:97 now
where the time goes in v1:
time: 417 us; the launch traced here: 416 us
  waiting for transfers between devices  237 us (57%)
  Pallas kernels  116 us (28%)
  local copies, waits for them, and re-layouts  27.4 us (7%)
  matrix products  17.2 us (4%)
  between operations  14.1 us (3%)
  other arithmetic  4.37 us (1%)
    all_gather x1, waiting for transfers between devices, local_fn(): lax.all_gather(tokens, 'sp', axis=0, tiled=True)  236 us
    pallas_call x1, Pallas kernels, attend(): pl.pallas_call(functools.partial(attend_kernel, proj_steps, blocks_dev, n...  116 us
    reshape x2, local copies, waits for them, and re-layouts, local_fn(): wq, wk, wv = (w.reshape(model, width) for w in (w_q, w_k, w_v))  24.7 us
    dot_general x3, matrix products, project(): jnp.dot(tokens, weight, preferred_element_type=jnp.float32)  17.2 us
  transfers between devices with their start and end apart: 1, of which 1 were waited for; matrix products, arithmetic and copies ran while one was open for 12% of the time, Pallas kernels for 0%

profile of v1, /device:TPU:97, one launch (start us, length us, event | category | flops | bytes accessed | tf_op | source)
XLA Modules:
  0.0 416.2 jit_solution(10931819010552209607)
XLA Ops:
  6.5 0.0 all-gather.2.cloned.1.call-start
  6.5 0.7 all-gather.2.cloned.1.call-update
  7.3 0.8 copy.39
  8.0 0.7 broadcast_compare_fusion
  8.7 0.1 copy.38
  8.8 0.7 add_select_fusion
  9.5 0.1 copy.37
  9.6 0.1 select_reduce_fusion.2
  9.7 0.6 fusion.6
  11.1 0.1 iota_compare_fusion.2
  11.2 0.1 add_select_fusion.2
  11.2 0.1 broadcast_in_dim.93
  11.3 0.7 select_n.74.bias_ref
  12.0 0.1 copy.40
  12.1 0.2 reduce-window.7
  12.3 0.1 add_reduce_fusion
  12.4 0.3 select_reduce_fusion.1
  12.8 0.1 copy.41
  12.9 0.7 select_select_fusion
  13.6 0.1 pad_add_fusion
  13.7 0.7 reshape.137.slots_ref
  14.3 12.3 %copy.42.wk_ref = bf16[2048,2048]{1,0:T(8,128)(2,1)} copy(bf16[2048,2048]{0,1:T(8,128)(2,1)} %bitcast.21) | data formatting | bytes 16777216 | tf_op jit(solution)/shard_map/reshape | solution.py:188
  26.7 12.4 %copy.43.wv_ref = bf16[2048,2048]{1,0:T(8,128)(2,1)} copy(bf16[2048,2048]{0,1:T(8,128)(2,1)} %bitcast.23) | data formatting | bytes 16777216 | tf_op jit(solution)/shard_map/reshape | solution.py:188
  39.1 0.1 select_reduce_fusion
  39.2 0.5 fusion.5.ids_ref
  39.7 0.0 copy-done
  39.7 6.9 %convolution_convert_fusion.1 = bf16[256,2048]{1,0:T(8,128)(2,1)} fusion(bf16[256,2048]{1,0:T(8,128)(2,1)S(1)} %copy-done, bf16[2048,2048]{0,1:T(8,128)(2,1)} %bitcast.22), kind=kOutput, calls=%fused_computation.1 | convolution fusion | flops 2148007936 | bytes 10485760 | tf_op jit(solution)/shard_map/dot_general | solution.py:192
  46.7 6.9 %convolution_convert_fusion = bf16[256,2048]{1,0:T(8,128)(2,1)} fusion(bf16[256,2048]{1,0:T(8,128)(2,1)S(1)} %copy-done, bf16[2048,2048]{0,1:T(8,128)(2,1)} %bitcast.24), kind=kOutput, calls=%fused_computation | convolution fusion | flops 2148007936 | bytes 10485760 | tf_op jit(solution)/shard_map/dot_general | solution.py:192
  53.5 0.0 slice-done.1
  53.5 3.4 convolution_convert_fusion.2.q_ref
  56.9 236.0 %all-gather.2.cloned.1.call-done = bf16[32768,2048]{1,0:T(8,128)(2,1)} async-done(((bf16[256,2048]{1,0:T(8,128)(2,1)}), bf16[32768,2048]{1,0:T(8,128)(2,1)}) %all-gather.2.cloned.1.call-update) | async-done | bytes 134217744 | tf_op jit(solution)/shard_map/all_gather | solution.py:186
  292.9 116.4 %attend.1 = bf16[256,2048]{1,0:T(8,128)(2,1)} custom-call(s32[56]{0:T(128)} %fusion.5.ids_ref, s32[1]{0:T(128)} %bitcast.1.count_ref, s32[64]{0:T(128)} %reshape.137.slots_ref, bf16[256,2048]{1,0:T(8,128)(2,1)} %convolution_convert_fusion.2.q_ref, f32[4,1,1024]{2,1,0:T(1,128)} %select_n.74.bias_ref, bf16[512,64,2048]{2,1,0:T(8,128)(2,1)} %bitcast.3.tok_ref, ...), custom_call_target="tpu_custom_call" | custom-call | flops 70000001024 | bytes 60000000 | tf_op jit(solution)/shard_map/attend/pallas_call | solution.py:165
  (13 shorter events, 0.0 us)
Async XLA Ops:
  6.5 286.4 %all-gather.2.cloned.1.call-start = ((), (), s32[]{:S(2)}) async-start(), calls=%async_computation | async-start | bytes 135266304 | tf_op jit(solution)/shard_map/all_gather | solution.py:186
  26.7 13.1 %copy-start = (bf16[256,2048]{1,0:T(8,128)(2,1)S(1)}, bf16[256,2048]{1,0:T(8,128)(2,1)}, u32[]{:S(2)}) copy-start(bf16[256,2048]{1,0:T(8,128)(2,1)} %param.6) | copy-start | bytes 3145732
  39.7 13.8 %slice-start = ((s8[8388608]{0:T(1024)(128)(4,1)}), s8[4194304]{0:T(1024)(128)(4,1)S(1)}, s32[]{:S(2)}) async-start(s8[8388608]{0:T(1024)(128)(4,1)} %bitcast.25), calls=%async_computation.1 | async-start | bytes 8388608
  46.6 6.9 %slice-start.1 = ((s8[8388608]{0:T(1024)(128)(4,1)}), s8[4194304]{0:T(1024)(128)(4,1)S(1)}, s32[]{:S(2)}) async-start(s8[8388608]{0:T(1024)(128)(4,1)} %bitcast.25), calls=%async_computation.2 | async-start | bytes 8388608
Sparse Core Ops, SparseCore 0:
  10.3 282.5 all-gather.1

commit v2 on v1

--- a/solution.py
+++ b/solution.py
@@ -10,7 +10,7 @@
 GLOB_BLOCKS = 2
 HEAD_GROUP = 4
 TILE_BLOCKS = 8
-COLS = 256
+COLS = 1024
 LOG2E = 1.4426950408889634
 
 
@@ -30,8 +30,8 @@
     def x_copy(at, g):
         return pltpu.make_async_copy(tok_ref.at[ids_ref[at * TILE_BLOCKS + g]], xbuf.at[lax.rem(at, 2), g], x_sem.at[lax.rem(at, 2), g])
 
-    def w_copy(src, which):
-        return pltpu.make_async_copy(src, wbuf.at[which], w_sem.at[which])
+    def w_copy(src, which, c):
+        return pltpu.make_async_copy(src.at[:, pl.ds(c * COLS, COLS)], wbuf.at[which, :, pl.ds(c * COLS, COLS)], w_sem.at[which, c])
 
     def near_copies():
         return (
@@ -43,8 +43,10 @@
     def _():
         for g in range(TILE_BLOCKS):
             x_copy(0, g).start()
-        w_copy(wk_ref, 0).start()
-        w_copy(wv_ref, 1).start()
+        for c in range(width // COLS):
+            w_copy(wk_ref, 0, c).start()
+        for c in range(width // COLS):
+            w_copy(wv_ref, 1, c).start()
         for copy in near_copies():
             copy.start()
 
@@ -53,8 +55,12 @@
         for g in range(TILE_BLOCKS):
             x_copy(step + 1, g).start()
 
-    def fill(pool, which):
+    def fill(pool, weight, which):
         def column(c, carry):
+            @pl.when(step == 0)
+            def _():
+                w_copy(weight, which, c).wait()
+
             at = pl.ds(pl.multiple_of(c * COLS, COLS), COLS)
             tok = xbuf[lax.rem(step, 2)].reshape(TILE_BLOCKS * block, -1)
             proj = jnp.dot(tok, wbuf[which, :, at], preferred_element_type=jnp.float32)
@@ -68,21 +74,13 @@
         for g in range(TILE_BLOCKS):
             x_copy(step, g).wait()
 
-        @pl.when(step == 0)
-        def _():
-            w_copy(wk_ref, 0).wait()
-
-        fill(kpool, 0)
-
-        @pl.when(step == 0)
-        def _():
-            w_copy(wv_ref, 1).wait()
-
-        fill(vpool, 1)
+        fill(kpool, wk_ref, 0)
+        fill(vpool, wv_ref, 1)
 
     @pl.when(step == proj_steps)
     def _():
-        w_copy(wo_ref, 0).start()
+        for c in range(width // COLS):
+            w_copy(wo_ref, 0, c).start()
         for copy in near_copies():
             copy.wait()
 
@@ -121,13 +119,12 @@
             ctx[pl.ds(pl.multiple_of(row * block, block), block), lanes] = picked.astype(jnp.bfloat16)
             return carry
 
-        lax.fori_loop(0, width // wide, heads, 0)
+        lax.fori_loop(0, width // wide, heads, 0, unroll=8)
 
     @pl.when(step == proj_steps + blocks_dev - 1)
     def _():
-        w_copy(wo_ref, 0).wait()
-
         def column(c, carry):
+            w_copy(wo_ref, 0, c).wait()
             at = pl.ds(pl.multiple_of(c * COLS, COLS), COLS)
             out_ref[:, at] = jnp.dot(ctx[...], wbuf[0, :, at], preferred_element_type=jnp.float32).astype(jnp.bfloat16)
             return carry
@@ -158,7 +155,7 @@
             pltpu.VMEM((2, model, width), jnp.bfloat16),
             pltpu.VMEM((blocks_dev * block, width), jnp.bfloat16),
             pltpu.SemaphoreType.DMA((2, TILE_BLOCKS)),
-            pltpu.SemaphoreType.DMA((2,)),
+            pltpu.SemaphoreType.DMA((2, width // COLS)),
             pltpu.SemaphoreType.DMA((2,)),
         ],
     )

time: 417 us -> 386 us (0.926)
  the two profiles are of different devices: /device:TPU:97 before, /device:TPU:104 now
where the time goes in v2:
time: 386 us; the launch traced here: 380 us
  waiting for transfers between devices  236 us (61%)
  Pallas kernels  80.9 us (21%)
  local copies, waits for them, and re-layouts  27.4 us (7%)
  matrix products  17.2 us (4%)
  between operations  14.1 us (4%)
  other arithmetic  4.37 us (1%)
    all_gather x1, waiting for transfers between devices, local_fn(): lax.all_gather(tokens, 'sp', axis=0, tiled=True)  235 us
    pallas_call x1, Pallas kernels, attend(): pl.pallas_call(functools.partial(attend_kernel, proj_steps, blocks_dev, n...  80.9 us
    reshape x2, local copies, waits for them, and re-layouts, local_fn(): wq, wk, wv = (w.reshape(model, width) for w in (w_q, w_k, w_v))  24.7 us
    dot_general x3, matrix products, project(): jnp.dot(tokens, weight, preferred_element_type=jnp.float32)  17.2 us
  transfers between devices with their start and end apart: 1, of which 1 were waited for; matrix products, arithmetic and copies ran while one was open for 13% of the time, Pallas kernels for 0%

profile of v2, /device:TPU:104, one launch (start us, length us, event | category | flops | bytes accessed | tf_op | source)
XLA Modules:
  0.0 380.2 jit_solution(12572880043620806476)
XLA Ops:
  6.5 0.0 all-gather.2.cloned.1.call-start
  6.5 0.7 all-gather.2.cloned.1.call-update
  7.3 0.8 copy.39
  8.0 0.7 broadcast_compare_fusion
  8.7 0.1 copy.38
  8.8 0.7 add_select_fusion
  9.5 0.1 copy.37
  9.6 0.1 select_reduce_fusion.2
  9.7 0.6 fusion.6
  11.1 0.1 iota_compare_fusion.2
  11.2 0.1 add_select_fusion.2
  11.2 0.1 broadcast_in_dim.93
  11.3 0.7 select_n.74.bias_ref
  12.0 0.1 copy.40
  12.1 0.2 reduce-window.7
  12.3 0.1 add_reduce_fusion
  12.4 0.3 select_reduce_fusion.1
  12.8 0.1 copy.41
  12.9 0.7 select_select_fusion
  13.6 0.1 pad_add_fusion
  13.7 0.7 reshape.137.slots_ref
  14.3 12.3 %copy.42.wk_ref = bf16[2048,2048]{1,0:T(8,128)(2,1)} copy(bf16[2048,2048]{0,1:T(8,128)(2,1)} %bitcast.21) | data formatting | bytes 16777216 | tf_op jit(solution)/shard_map/reshape | solution.py:185
  26.7 12.4 %copy.43.wv_ref = bf16[2048,2048]{1,0:T(8,128)(2,1)} copy(bf16[2048,2048]{0,1:T(8,128)(2,1)} %bitcast.23) | data formatting | bytes 16777216 | tf_op jit(solution)/shard_map/reshape | solution.py:185
  39.1 0.1 select_reduce_fusion
  39.2 0.5 fusion.5.ids_ref
  39.7 0.0 copy-done
  39.7 6.9 %convolution_convert_fusion.1 = bf16[256,2048]{1,0:T(8,128)(2,1)} fusion(bf16[256,2048]{1,0:T(8,128)(2,1)S(1)} %copy-done, bf16[2048,2048]{0,1:T(8,128)(2,1)} %bitcast.22), kind=kOutput, calls=%fused_computation.1 | convolution fusion | flops 2148007936 | bytes 10485760 | tf_op jit(solution)/shard_map/dot_general | solution.py:189
  46.6 6.9 %convolution_convert_fusion = bf16[256,2048]{1,0:T(8,128)(2,1)} fusion(bf16[256,2048]{1,0:T(8,128)(2,1)S(1)} %copy-done, bf16[2048,2048]{0,1:T(8,128)(2,1)} %bitcast.24), kind=kOutput, calls=%fused_computation | convolution fusion | flops 2148007936 | bytes 10485760 | tf_op jit(solution)/shard_map/dot_general | solution.py:189
  53.5 0.0 slice-done.1
  53.5 3.4 convolution_convert_fusion.2.q_ref
  56.9 235.5 %all-gather.2.cloned.1.call-done = bf16[32768,2048]{1,0:T(8,128)(2,1)} async-done(((bf16[256,2048]{1,0:T(8,128)(2,1)}), bf16[32768,2048]{1,0:T(8,128)(2,1)}) %all-gather.2.cloned.1.call-update) | async-done | bytes 134217744 | tf_op jit(solution)/shard_map/all_gather | solution.py:183
  292.4 80.9 %attend.1 = bf16[256,2048]{1,0:T(8,128)(2,1)} custom-call(s32[56]{0:T(128)} %fusion.5.ids_ref, s32[1]{0:T(128)} %bitcast.1.count_ref, s32[64]{0:T(128)} %reshape.137.slots_ref, bf16[256,2048]{1,0:T(8,128)(2,1)} %convolution_convert_fusion.2.q_ref, f32[4,1,1024]{2,1,0:T(1,128)} %select_n.74.bias_ref, bf16[512,64,2048]{2,1,0:T(8,128)(2,1)} %bitcast.3.tok_ref, ...), custom_call_target="tpu_custom_call" | custom-call | flops 70000001024 | bytes 60000000 | tf_op jit(solution)/shard_map/attend/pallas_call | solution.py:162
  (13 shorter events, 0.0 us)
Async XLA Ops:
  6.5 285.9 %all-gather.2.cloned.1.call-start = ((), (), s32[]{:S(2)}) async-start(), calls=%async_computation | async-start | bytes 135266304 | tf_op jit(solution)/shard_map/all_gather | solution.py:183
  26.7 13.1 %copy-start = (bf16[256,2048]{1,0:T(8,128)(2,1)S(1)}, bf16[256,2048]{1,0:T(8,128)(2,1)}, u32[]{:S(2)}) copy-start(bf16[256,2048]{1,0:T(8,128)(2,1)} %param.6) | copy-start | bytes 3145732
  39.7 13.8 %slice-start = ((s8[8388608]{0:T(1024)(128)(4,1)}), s8[4194304]{0:T(1024)(128)(4,1)S(1)}, s32[]{:S(2)}) async-start(s8[8388608]{0:T(1024)(128)(4,1)} %bitcast.25), calls=%async_computation.1 | async-start | bytes 8388608
  46.6 6.9 %slice-start.1 = ((s8[8388608]{0:T(1024)(128)(4,1)}), s8[4194304]{0:T(1024)(128)(4,1)S(1)}, s32[]{:S(2)}) async-start(s8[8388608]{0:T(1024)(128)(4,1)} %bitcast.25), calls=%async_computation.2 | async-start | bytes 8388608
Sparse Core Ops, SparseCore 0:
  10.3 282.0 all-gather.1
